TPU v7x, 32 devices: a whole 2x2x4 slice. The times are simulated.
32 devices in a mesh: groups: 2 (over y), block: 4 (over z), seg: 2 (over x), sub: 2 (over core).
Axes of the slice: x: 2, y: 2, z: 4, core: 2. Of those that a mesh axis runs over, the one named last changes fastest.
Arguments:
- old_fields: float32 [2048, 4, 512], P(('groups', 'block', 'seg', 'sub')), parts along dimension 0, may hold values from -6 to 6
- corner_shift: float32 [24, 2048], P(None, ('groups', 'block', 'seg', 'sub')), parts along dimension 1, may hold values from -0.2 to 0.2
- targets: float32 [3, 131072], P(None, ('groups', 'block', 'seg', 'sub')), parts along dimension 1, may hold values from -0.7 to 0.7
- owners: int32 [1024], P(('groups', 'block', 'seg', 'sub')), parts along dimension 0, may hold values from 0 to 1023, as said below
Outputs:
- new_fields: float32 [4, 131072], P(None, ('groups', 'block', 'seg', 'sub')), parts along dimension 1
There are 2 independent parts, one for each index of `groups`. A program takes and returns all parts, laid end to end along the dimension named above; each array names one. Nothing has to cross between parts.
Inputs may be any that keep to these rules, and one draw needn't show every extreme that they name: `owners`: owner e lies on device e // 64. At most 2 of the blocks on the rows of one device are owned by elements of any one device, and in every draw some device owns exactly 2 blocks of every device.
All inputs are finite; a program needn't handle non-finite values.
Results may differ from a plain program's by a relative error of at most 0.00029.
Values sent between devices are 32-bit elements; how exact they have to be, the bound alone decides.
A program may use at most 64 MiB of HBM per device.

v0:
```python
import jax
import jax.numpy as jnp
import numpy as np
from jax import lax
from jax.sharding import PartitionSpec as P

NEWTON = 3
CAP = 2


GLL_POINTS = (
    -1.0,
    -0.8717401485096066,
    -0.5917001814331423,
    -0.2092992179024789,
    0.2092992179024789,
    0.5917001814331423,
    0.8717401485096066,
    1.0,
)
EXACT = lax.Precision.HIGHEST


def lagrange_rows(coords):
    gll_nodes = jnp.array(GLL_POINTS, jnp.float32)
    offsets = coords[None, :] - gll_nodes[:, None]
    spacing = gll_nodes[:, None] - gll_nodes[None, :] + jnp.eye(8, dtype=jnp.float32)
    diag_mask = jnp.eye(8, dtype=bool)
    factors = jnp.where(diag_mask[:, :, None], 1.0, offsets[None, :, :] / spacing[:, :, None])
    return jnp.prod(factors, axis=1)


def corner_signs():
    bit_table = np.array(
        [[corner >> 2 - coord_dim & 1 for corner in range(8)] for coord_dim in range(3)], np.float32
    )
    return jnp.asarray(2.0 * bit_table - 1.0)


def outer_prod(first, second, third):
    return (first[:, None, None, :] * second[None, :, None, :] * third[None, None, :, :]).reshape(
        8, -1
    )


def trilinear(ref_pos):
    shape_list = []
    slope_list = []
    for coord_dim in range(3):
        coordinate = ref_pos[coord_dim]
        shape_list.append(jnp.stack([0.5 - 0.5 * coordinate, 0.5 + 0.5 * coordinate]))
        slope_list.append(
            jnp.stack([jnp.full_like(coordinate, -0.5), jnp.full_like(coordinate, 0.5)])
        )
    values = outer_prod(shape_list[0], shape_list[1], shape_list[2])
    slopes = [
        outer_prod(slope_list[0], shape_list[1], shape_list[2]),
        outer_prod(shape_list[0], slope_list[1], shape_list[2]),
        outer_prod(shape_list[0], shape_list[1], slope_list[2]),
    ]
    return (values, slopes)


def solve_three(matrix, rhs_rows):
    cofactors = []
    for row_id in range(3):
        keep_rows = [remain for remain in range(3) if remain != row_id]
        cof_row = []
        for col_id in range(3):
            keep_cols = [remain for remain in range(3) if remain != col_id]
            sign_factor = 1.0 if (row_id + col_id) % 2 == 0 else -1.0
            cof_row.append(
                sign_factor
                * (
                    matrix[keep_rows[0]][keep_cols[0]] * matrix[keep_rows[1]][keep_cols[1]]
                    - matrix[keep_rows[0]][keep_cols[1]] * matrix[keep_rows[1]][keep_cols[0]]
                )
            )
        cofactors.append(cof_row)
    determinant = (
        matrix[0][0] * cofactors[0][0]
        + matrix[0][1] * cofactors[0][1]
        + matrix[0][2] * cofactors[0][2]
    )
    return [
        (
            cofactors[0][col_id] * rhs_rows[0]
            + cofactors[1][col_id] * rhs_rows[1]
            + cofactors[2][col_id] * rhs_rows[2]
        )
        / determinant
        for col_id in range(3)
    ]


def invert_map(corners, target):
    ref_pos = jnp.zeros_like(target)
    for iteration in range(NEWTON):
        values, slopes = trilinear(ref_pos)
        mapped = jnp.dot(corners, values, precision=EXACT)
        columns = [jnp.dot(corners, slope_row, precision=EXACT) for slope_row in slopes]
        matrix = [[columns[col_id][row_id] for col_id in range(3)] for row_id in range(3)]
        misfit = mapped - target
        update = solve_three(matrix, [misfit[row_id] for row_id in range(3)])
        ref_pos = jnp.clip(ref_pos - jnp.stack(update), -1.2, 1.2)
    return ref_pos


def interpolate(element_field, corners, target):
    ref_pos = invert_map(corners, target)
    along_x = lagrange_rows(ref_pos[0])
    along_y = lagrange_rows(ref_pos[1])
    along_z = lagrange_rows(ref_pos[2])
    weights = (along_y[:, None, :] * along_z[None, :, :]).reshape(64, -1)
    var_count = element_field.shape[0]
    partial_sum = jnp.dot(element_field.reshape(var_count * 8, 64), weights, precision=EXACT)
    return jnp.sum(partial_sum.reshape(var_count, 8, -1) * along_x[None, :, :], axis=1)


def interpolate_blocks(fields, shifts, points):
    cube_signs = corner_signs()

    def per_block(inputs):
        element_field, shift_row, target = inputs
        return interpolate(element_field, cube_signs + shift_row.reshape(3, 8), target)

    return lax.map(per_block, (fields, shifts, points), batch_size=64)


def slot_table(owners, elems_local, capacity):
    owner_dev = owners // elems_local
    local_elem = owners - owner_dev * elems_local
    block_count = owners.shape[0]
    earlier = jnp.tril(jnp.ones((block_count, block_count), jnp.int32), -1)
    matches = (owner_dev[:, None] == owner_dev[None, :]).astype(jnp.int32)
    arrival = jnp.sum(matches * earlier, axis=1)
    return (owner_dev * capacity + arrival, local_elem)


def shards(old_fields, corner_shift, targets, owners):
    outer_count = lax.axis_size("block")
    inner_count = lax.axis_size("seg") * lax.axis_size("sub")
    slot_count = outer_count * inner_count * CAP
    elems_local = old_fields.shape[0]
    var_count = old_fields.shape[1]
    block_count = owners.shape[0]
    slot_index, local_elem = slot_table(owners, elems_local, CAP)
    block_points = targets.reshape(3, block_count, -1).transpose(1, 0, 2)
    point_count = block_points.shape[2]
    outgoing = jnp.zeros((slot_count, 3, point_count), jnp.float32).at[slot_index].set(block_points)
    wanted = jnp.full((slot_count,), -1, jnp.int32).at[slot_index].set(local_elem)
    arrived, asked = (
        lax.all_to_all(
            lax.all_to_all(
                outgoing.reshape(outer_count, inner_count, CAP, 3, point_count),
                "block",
                split_axis=0,
                concat_axis=0,
                tiled=True,
            ),
            ("seg", "sub"),
            split_axis=1,
            concat_axis=1,
            tiled=True,
        ),
        lax.all_to_all(
            lax.all_to_all(
                wanted.reshape(outer_count, inner_count, CAP),
                "block",
                split_axis=0,
                concat_axis=0,
                tiled=True,
            ),
            ("seg", "sub"),
            split_axis=1,
            concat_axis=1,
            tiled=True,
        ),
    )
    asked = asked.reshape(slot_count)
    live_slot = asked >= 0
    element = jnp.where(live_slot, asked, 0)
    fields = old_fields[element]
    shifts = jnp.transpose(corner_shift[:, element])
    computed = interpolate_blocks(fields, shifts, arrived.reshape(slot_count, 3, point_count))
    computed = jnp.where(live_slot[:, None, None], computed, 0.0)
    returned = lax.all_to_all(
        lax.all_to_all(
            computed.reshape(outer_count, inner_count, CAP, var_count, point_count),
            "block",
            split_axis=0,
            concat_axis=0,
            tiled=True,
        ),
        ("seg", "sub"),
        split_axis=1,
        concat_axis=1,
        tiled=True,
    )
    mine = returned.reshape(slot_count, var_count, point_count)[slot_index]
    return mine.transpose(1, 0, 2).reshape(var_count, -1)


def solution(mesh):
    in_specs = (
        P(("groups", "block", "seg", "sub"), None, None),
        P(None, ("groups", "block", "seg", "sub")),
        P(None, ("groups", "block", "seg", "sub")),
        P(("groups", "block", "seg", "sub")),
    )
    out_specs = P(None, ("groups", "block", "seg", "sub"))
    return jax.shard_map(shards, mesh=mesh, in_specs=in_specs, out_specs=out_specs, check_vma=False)
```

profile of v0, /device:TPU:0, one launch (start us, length us, event | category | flops | bytes accessed | tf_op | source)
XLA Modules:
  0.0 64.6 jit_solution(12692678252523733216)
XLA Ops:
  0.0 0.7 %multiply_subtract_fusion.2 = (s32[32]{0:T(128)S(1)}, s32[32]{0:T(128)S(1)}, s32[32]{0:T(128)S(1)}) fusion(s32[32]{0:T(128)} %param.11), kind=kLoop, calls=%fused_computation.237 | loop fusion | flops 576 | bytes 512 | tf_op jit(solution)/shard_map/sub | solution.py:132
  0.9 0.7 %scatter_custom_fusion = s32[32]{0:T(128)S(1)} fusion(s32[32]{0:T(128)S(1)} %compare_select_fusion.2, s32[32]{0:T(128)S(1)} %get-tuple-element.10, s32[]{:T(128)} %constant.26.clone.1), kind=kCustom, calls=%fused_computation.239 | custom fusion | bytes 132 | tf_op jit(solution)/shard_map/scatter | solution.py:151
  1.7 0.7 %copy.272 = s32[4,4,2]{1,2,0:T(2,128)} copy(s32[4,4,2]{2,1,0:T(4,128)S(1)} %reshape.2161) | data formatting | bytes 256 | tf_op jit(solution)/shard_map/reshape | solution.py:168
  2.4 6.5 %all-to-all-start = ((s32[4,4,2]{1,2,0:T(2,128)}), s32[4,4,2]{1,2,0:T(2,128)S(1)}, u32[]{:S(2)}, u32[]{:S(2)}) async-start(s32[4,4,2]{1,2,0:T(2,128)} %copy.272), calls=%async_computation | async-start | bytes 8192 | tf_op jit(solution)/shard_map/all_to_all | solution.py:167
  9.1 1.5 %scatter_fusion = f32[32,3,128]{2,1,0:T(4,128)S(1)} fusion(f32[32,3,128]{2,1,0:T(4,128)S(1)} %broadcast.569, s32[32]{0:T(128)S(1)} %compare_select_fusion.2, f32[32,3,128]{2,1,0:T(4,128)S(1)} %bitcast.790), kind=kCustom, calls=%fused_computation.4 | custom fusion | bytes 147584 | tf_op jit(solution)/shard_map/scatter | solution.py:150
  10.6 3.9 %all-to-all-done = s32[4,4,2]{1,2,0:T(2,128)S(1)} async-done(((s32[4,4,2]{1,2,0:T(2,128)}), s32[4,4,2]{1,2,0:T(2,128)S(1)}, u32[]{:S(2)}, u32[]{:S(2)}) %all-to-all-start) | async-done | bytes 160 | tf_op jit(solution)/shard_map/all_to_all | solution.py:167
  14.5 0.7 %copy.273 = s32[4,4,2]{0,2,1:T(2,128)} copy(s32[4,4,2]{1,2,0:T(2,128)S(1)} %all-to-all-done) | data formatting | bytes 256 | tf_op jit(solution)/shard_map/all_to_all | solution.py:167
  15.2 3.2 %all-to-all-start.1 = ((s32[4,4,2]{0,2,1:T(2,128)}), s32[4,4,2]{0,2,1:T(2,128)S(1)}, u32[]{:S(2)}, u32[]{:S(2)}) async-start(s32[4,4,2]{0,2,1:T(2,128)} %copy.273), calls=%async_computation.1 | async-start | bytes 8192 | tf_op jit(solution)/shard_map/all_to_all | solution.py:166
  18.4 0.6 %copy.281 = f32[4,4,2,3,128]{4,2,1,3,0:T(2,128)} copy(f32[4,4,2,3,128]{4,3,2,1,0:T(4,128)S(1)} %bitcast.767) | data formatting | bytes 98304 | tf_op jit(solution)/shard_map/reshape | solution.py:155
  19.1 3.1 %all-to-all-done.1 = s32[4,4,2]{0,2,1:T(2,128)S(1)} async-done(((s32[4,4,2]{0,2,1:T(2,128)}), s32[4,4,2]{0,2,1:T(2,128)S(1)}, u32[]{:S(2)}, u32[]{:S(2)}) %all-to-all-start.1) | async-done | bytes 160 | tf_op jit(solution)/shard_map/all_to_all | solution.py:166
  22.2 3.3 %all-to-all-start.2 = ((f32[4,4,2,3,128]{4,2,1,3,0:T(2,128)}), f32[4,4,2,3,128]{4,2,1,3,0:T(2,128)S(1)}, u32[]{:S(2)}, u32[]{:S(2)}) async-start(f32[4,4,2,3,128]{4,2,1,3,0:T(2,128)} %copy.281), calls=%async_computation.2 | async-start | bytes 98304 | tf_op jit(solution)/shard_map/all_to_all | solution.py:154
  26.9 0.7 %copy-done.6 = f32[24]{0:T(128)S(1)} copy-done((f32[24]{0:T(128)S(1)}, f32[24]{0:T(128)}, u32[]{:S(2)}) %copy-start.6) | copy-done | bytes 120
  29.1 2.0 %all-to-all-done.2 = f32[4,4,2,3,128]{4,2,1,3,0:T(2,128)S(1)} async-done(((f32[4,4,2,3,128]{4,2,1,3,0:T(2,128)}), f32[4,4,2,3,128]{4,2,1,3,0:T(2,128)S(1)}, u32[]{:S(2)}, u32[]{:S(2)}) %all-to-all-start.2) | async-done | bytes 49184 | tf_op jit(solution)/shard_map/all_to_all | solution.py:154
  31.1 0.6 copy.282
  31.8 3.3 %all-to-all-start.3 = ((f32[4,4,2,3,128]{4,2,0,3,1:T(2,128)}), f32[4,4,2,3,128]{4,2,0,3,1:T(2,128)S(1)}, u32[]{:S(2)}, u32[]{:S(2)}) async-start(f32[4,4,2,3,128]{4,2,0,3,1:T(2,128)} %copy.282), calls=%async_computation.3 | async-start | bytes 98304 | tf_op jit(solution)/shard_map/all_to_all | solution.py:153
  35.2 0.7 %gather_fusion = f32[32,4,512]{2,1,0:T(4,128)S(1)} fusion(f32[64,4,512]{2,1,0:T(4,128)S(1)} %copy-done, s32[1024]{0:T(1024)S(1)} %pad_clamp_fusion.1), kind=kCustom, calls=%fused_computation | custom fusion | bytes 524416 | tf_op jit(solution)/shard_map/gather | solution.py:183
  36.2 2.8 %all-to-all-done.3 = f32[4,4,2,3,128]{4,2,0,3,1:T(2,128)S(1)} async-done(((f32[4,4,2,3,128]{4,2,0,3,1:T(2,128)}), f32[4,4,2,3,128]{4,2,0,3,1:T(2,128)S(1)}, u32[]{:S(2)}, u32[]{:S(2)}) %all-to-all-start.3) | async-done | bytes 49184 | tf_op jit(solution)/shard_map/all_to_all | solution.py:153
  44.4 1.1 %fusion.4 = (f32[32,8,128]{2,1,0:T(8,128)S(1)}, f32[32,8,128]{2,1,0:T(8,128)S(1)}, f32[32,8,128]{2,1,0:T(8,128)S(1)}) fusion(f32[32,8,128]{2,1,0:T(8,128)S(1)} %get-tuple-element.61, f32[8,8]{1,0:T(8,128)S(1)} %add_add_fusion, pred[8,8]{1,0:T(8,128)(4,1)S(1)} %iota_compare_fusion.1, f32[32,8,128]{2,1,0:T(8,128)S(1)} %get-tuple-element.60, ...), kind=kLoop, calls=%fused_computation.14 | loop fusion | flops 2260992 | bytes 786752 | tf_op jit(solution)/shard_map/vmap()/reduce_prod | solution.py:30
  45.4 1.1 %fusion.1 = f32[32,4,128]{2,1,0:T(4,128)S(1)} fusion(f32[32,32,64]{2,1,0:T(8,128)S(1)} %reshape.2163, f32[32,8,128]{2,1,0:T(8,128)S(1)} %get-tuple-element.6, f32[32,8,128]{2,1,0:T(8,128)S(1)} %get-tuple-element.7, f32[32,8,128]{2,1,0:T(8,128)S(1)} %get-tuple-element.5), kind=kOutput, calls=%fused_computation.7 | convolution fusion | flops 101171200 | bytes 720896 | tf_op jit(solution)/shard_map/vmap()/dot_general | solution.py:116
  46.7 8.6 %all_to_all.30 = f32[4,4,2,4,128]{4,2,1,3,0:T(2,128)S(1)} all-to-all(f32[4,4,2,4,128]{4,2,1,3,0:T(2,128)S(1)} %copy.319), channel_id=1, replica_groups=mesh['groups'=2,'block'=4,'seg'=2,'sub'=2] {'block'}, dimensions={0} | all-to-all | bytes 131072 | tf_op jit(solution)/shard_map/all_to_all | solution.py:188
  55.3 0.6 %copy.320 = f32[4,4,2,4,128]{4,3,2,0,1:T(4,128)} copy(f32[4,4,2,4,128]{4,2,1,3,0:T(2,128)S(1)} %all_to_all.30) | data formatting | bytes 131072 | tf_op jit(solution)/shard_map/all_to_all | solution.py:188
  56.0 3.3 %all-to-all-start.5 = ((f32[4,4,2,4,128]{4,3,2,0,1:T(4,128)}), f32[4,4,2,4,128]{4,3,2,0,1:T(4,128)S(1)}, u32[]{:S(2)}, u32[]{:S(2)}) async-start(f32[4,4,2,4,128]{4,3,2,0,1:T(4,128)} %copy.320), calls=%async_computation.5 | async-start | bytes 131072 | tf_op jit(solution)/shard_map/all_to_all | solution.py:187
  59.3 4.1 %all-to-all-done.5 = f32[4,4,2,4,128]{4,3,2,0,1:T(4,128)S(1)} async-done(((f32[4,4,2,4,128]{4,3,2,0,1:T(4,128)}), f32[4,4,2,4,128]{4,3,2,0,1:T(4,128)S(1)}, u32[]{:S(2)}, u32[]{:S(2)}) %all-to-all-start.5) | async-done | bytes 65568 | tf_op jit(solution)/shard_map/all_to_all | solution.py:187
  63.4 1.2 %gather_fusion.2 = f32[32,4,128]{2,1,0:T(4,128)} fusion(f32[32,4,128]{2,1,0:T(4,128)S(1)} %bitcast.769, s32[1024]{0:T(1024)S(1)} %pad_clamp_fusion), kind=kCustom, calls=%fused_computation.2 | custom fusion | bytes 131200 | tf_op jit(solution)/shard_map/gather | solution.py:200
  (99 shorter events, 8.9 us)
Async XLA Ops:
  0.0 35.1 %copy-start = (f32[64,4,512]{2,1,0:T(4,128)S(1)}, f32[64,4,512]{2,1,0:T(4,128)}, u32[]{:S(2)}) copy-start(f32[64,4,512]{2,1,0:T(4,128)} %param.8) | copy-start | bytes 1572868
  1.7 7.2 %copy-start.3 = (f32[24,64]{1,0:T(8,128)S(1)}, f32[24,64]{1,0:T(8,128)}, u32[]{:S(2)}) copy-start(f32[24,64]{1,0:T(8,128)} %param.9) | copy-start | bytes 18436
  1.7 7.3 %copy-start.7 = (f32[8]{0:T(128)S(1)}, f32[8]{0:T(128)}, u32[]{:S(2)}) copy-start(f32[8]{0:T(128)} %constant.77) | copy-start | bytes 100
  1.7 7.3 %copy-start.8 = (f32[8]{0:T(128)S(1)}, f32[8]{0:T(128)}, u32[]{:S(2)}) copy-start(f32[8]{0:T(128)} %constant.75.clone) | copy-start | bytes 100
  2.4 6.7 %copy-start.1 = (f32[3,4096]{1,0:T(4,128)S(1)}, f32[3,4096]{1,0:T(4,128)}, u32[]{:S(2)}) copy-start(f32[3,4096]{1,0:T(4,128)} %param.10) | copy-start | bytes 147460
  2.4 12.1 %all-to-all-start = ((s32[4,4,2]{1,2,0:T(2,128)}), s32[4,4,2]{1,2,0:T(2,128)S(1)}, u32[]{:S(2)}, u32[]{:S(2)}) async-start(s32[4,4,2]{1,2,0:T(2,128)} %copy.272), calls=%async_computation | async-start | bytes 8192 | tf_op jit(solution)/shard_map/all_to_all | solution.py:167
  15.2 7.0 %all-to-all-start.1 = ((s32[4,4,2]{0,2,1:T(2,128)}), s32[4,4,2]{0,2,1:T(2,128)S(1)}, u32[]{:S(2)}, u32[]{:S(2)}) async-start(s32[4,4,2]{0,2,1:T(2,128)} %copy.273), calls=%async_computation.1 | async-start | bytes 8192 | tf_op jit(solution)/shard_map/all_to_all | solution.py:166
  22.2 8.9 %all-to-all-start.2 = ((f32[4,4,2,3,128]{4,2,1,3,0:T(2,128)}), f32[4,4,2,3,128]{4,2,1,3,0:T(2,128)S(1)}, u32[]{:S(2)}, u32[]{:S(2)}) async-start(f32[4,4,2,3,128]{4,2,1,3,0:T(2,128)} %copy.281), calls=%async_computation.2 | async-start | bytes 98304 | tf_op jit(solution)/shard_map/all_to_all | solution.py:154
  26.3 0.7 %copy-start.4 = (f32[2,128]{1,0:T(2,128)S(1)}, f32[2,128]{1,0:T(2,128)}, u32[]{:S(2)}) copy-start(f32[2,128]{1,0:T(2,128)} %constant.68.clone.1) | copy-start | bytes 3076
  26.9 0.7 %copy-start.6 = (f32[24]{0:T(128)S(1)}, f32[24]{0:T(128)}, u32[]{:S(2)}) copy-start(f32[24]{0:T(128)} %constant.76) | copy-start | bytes 292
  28.3 0.7 %copy-start.5 = (f32[3,8]{1,0:T(4,128)S(1)}, f32[3,8]{1,0:T(4,128)}, u32[]{:S(2)}) copy-start(f32[3,8]{1,0:T(4,128)} %constant.74.clone) | copy-start | bytes 292
  31.8 7.3 %all-to-all-start.3 = ((f32[4,4,2,3,128]{4,2,0,3,1:T(2,128)}), f32[4,4,2,3,128]{4,2,0,3,1:T(2,128)S(1)}, u32[]{:S(2)}, u32[]{:S(2)}) async-start(f32[4,4,2,3,128]{4,2,0,3,1:T(2,128)} %copy.282), calls=%async_computation.3 | async-start | bytes 98304 | tf_op jit(solution)/shard_map/all_to_all | solution.py:153
  39.6 0.7 %copy-start.2 = (f32[2,128]{1,0:T(2,128)S(1)}, f32[2,128]{1,0:T(2,128)}, u32[]{:S(2)}) copy-start(f32[2,128]{1,0:T(2,128)} %constant.73.clone.1) | copy-start | bytes 3076
  56.0 7.4 %all-to-all-start.5 = ((f32[4,4,2,4,128]{4,3,2,0,1:T(4,128)}), f32[4,4,2,4,128]{4,3,2,0,1:T(4,128)S(1)}, u32[]{:S(2)}, u32[]{:S(2)}) async-start(f32[4,4,2,4,128]{4,3,2,0,1:T(4,128)} %copy.320), calls=%async_computation.5 | async-start | bytes 131072 | tf_op jit(solution)/shard_map/all_to_all | solution.py:187
where the time goes:
time: 65.3 us; the launch traced here: 64.6 us
  starting transfers between devices  19.6 us (30%)
  waiting for transfers between devices  15.9 us (24%)
  local copies, waits for them, and re-layouts  12 us (18%)
  blocking collectives  8.63 us (13%)
  matrix products  5.16 us (8%)
  other arithmetic  2.71 us (4%)
    all_to_all x1, blocking collectives, shards(): lax.all_to_all(computed.reshape(outer_count, inner_count, CAP, var_count,...  8.63 us
    all_to_all x1, starting transfers between devices, shards(): lax.all_to_all(wanted.reshape(outer_count, inner_count, CAP), 'block', sp...  6.48 us
    all_to_all x1, waiting for transfers between devices, shards(): lax.all_to_all(lax.all_to_all(computed.reshape(outer_count, inner_count,...  4.07 us
    all_to_all x1, waiting for transfers between devices, shards(): lax.all_to_all(wanted.reshape(outer_count, inner_count, CAP), 'block', sp...  3.88 us
    all_to_all x1, starting transfers between devices, shards(): lax.all_to_all(lax.all_to_all(computed.reshape(outer_count, inner_count,...  3.28 us
    all_to_all x1, starting transfers between devices, shards(): lax.all_to_all(outgoing.reshape(outer_count, inner_count, CAP, 3, point_c...  3.27 us
    all_to_all x1, starting transfers between devices, shards(): lax.all_to_all(lax.all_to_all(outgoing.reshape(outer_count, inner_count,...  3.27 us
    all_to_all x1, starting transfers between devices, shards(): lax.all_to_all(lax.all_to_all(wanted.reshape(outer_count, inner_count, CA...  3.24 us
  transfers between devices with their start and end apart: 5, of which 5 were waited for; matrix products, arithmetic and copies ran while one was open for 8% of the time, Pallas kernels for 0%

commit v1 on v0

v1 whole, which is shorter than its diff:
```python
import functools

import jax
import jax.numpy as jnp
from jax import lax
from jax.experimental import pallas as pl
from jax.experimental.pallas import tpu as pltpu
from jax.sharding import PartitionSpec as P

NEWTON = 3
CAP = 2
GROUP_PEERS = 8
AXES = ("block", "seg", "sub")

GLL_POINTS = (
    -1.0,
    -0.8717401485096066,
    -0.5917001814331423,
    -0.2092992179024789,
    0.2092992179024789,
    0.5917001814331423,
    0.8717401485096066,
    1.0,
)
WEIGHTS = []
for _n in range(8):
    _w = 1.0
    for _m in range(8):
        if _m != _n:
            _w /= GLL_POINTS[_n] - GLL_POINTS[_m]
    WEIGHTS.append(_w)

F32 = jnp.float32
BF16 = jnp.bfloat16
EXACT = lax.Precision.HIGHEST
NT = (((1,), (1,)), ((), ()))


def iota(shape, dim):
    return lax.broadcasted_iota(jnp.int32, shape, dim)


def flip(index, static):
    bit = 1
    while bit <= static:
        if static & bit:
            index = index + bit * (1 - 2 * ((index // bit) % 2))
        bit *= 2
    return index


def newton(coef, y):
    def update(xi, jac, misfit):
        m = jac
        cof = [
            [m[1][1] * m[2][2] - m[1][2] * m[2][1], m[1][2] * m[2][0] - m[1][0] * m[2][2], m[1][0] * m[2][1] - m[1][1] * m[2][0]],
            [m[0][2] * m[2][1] - m[0][1] * m[2][2], m[0][0] * m[2][2] - m[0][2] * m[2][0], m[0][1] * m[2][0] - m[0][0] * m[2][1]],
            [m[0][1] * m[1][2] - m[0][2] * m[1][1], m[0][2] * m[1][0] - m[0][0] * m[1][2], m[0][0] * m[1][1] - m[0][1] * m[1][0]],
        ]
        inv = 1.0 / (m[0][0] * cof[0][0] + m[0][1] * cof[0][1] + m[0][2] * cof[0][2])
        out = []
        for b in range(3):
            step = (cof[0][b] * misfit[0] + cof[1][b] * misfit[1] + cof[2][b] * misfit[2]) * inv
            new = -step if xi is None else xi[b] - step
            out.append(jnp.clip(new, -1.2, 1.2))
        return out

    xi = update(None, [[c[4], c[2], c[1]] for c in coef], [c[0] - t for c, t in zip(coef, y)])
    for _ in range(NEWTON - 1):
        u, v, w = xi
        uv, uw, vw = u * v, u * w, v * w
        jac, misfit = [], []
        for c, t in zip(coef, y):
            du = c[4] + c[6] * v + c[5] * w + c[7] * vw
            dv = c[2] + c[6] * u + c[3] * w + c[7] * uw
            dw = c[1] + c[5] * u + c[3] * v + c[7] * uv
            jac.append([du, dv, dw])
            misfit.append((c[0] - t) + u * du + v * (c[2] + c[3] * w) + w * c[1])
        xi = update(xi, jac, misfit)
    return xi


def lagrange(x):
    diff = [x - t for t in GLL_POINTS]
    pre = [None, diff[0]]
    for n in range(2, 8):
        pre.append(pre[-1] * diff[n - 1])
    suf = [None] * 8
    suf[6] = diff[7]
    for n in range(5, -1, -1):
        suf[n] = suf[n + 1] * diff[n + 1]
    out = []
    for n in range(8):
        value = suf[n] if n == 0 else pre[n] if n == 7 else pre[n] * suf[n]
        out.append(value * WEIGHTS[n])
    return out


def kernel(sizes, group_peers, owners_ref, targets_ref, shift_ref, fields_hbm, out_ref,
           fbuf, table, send, recv, res, ret, lag, idsend, idrecv, ids, slotv, slots,
           fsem, idsem, idsem2, slotsem, s0, r0, s1, r1, s2, r2):
    nb, ns, nc = sizes
    n = nb * ns * nc
    blocks = owners_ref.shape[1]
    elems = shift_ref.shape[1]
    pts = out_ref.shape[2]
    groups = n // group_peers
    lanes = idsend.shape[1]
    here = [lax.axis_index(a) for a in AXES]
    me = (here[0] * ns + here[1]) * nc + here[2]

    def peer(k):
        if isinstance(k, int):
            return {
                "block": flip(here[0], k // (ns * nc)),
                "seg": flip(here[1], (k // nc) % ns),
                "sub": flip(here[2], k % nc),
            }
        other = jnp.bitwise_xor(me, k)
        return {"block": other // (ns * nc), "seg": (other // nc) % ns, "sub": other % nc}

    def rows(k, count=1):
        start = 8 * k
        return pl.ds(start if isinstance(start, int) else pl.multiple_of(start, 8), 8 * count)

    def remote(src, dst, ssem, rsem, k, g):
        part = rows(k) if src is send else pl.ds(CAP * k, CAP)
        return pltpu.make_async_remote_copy(
            src_ref=src.at[part], dst_ref=dst.at[part],
            send_sem=ssem, recv_sem=rsem.at[g],
            device_id=peer(k), device_id_type=pl.DeviceIdType.MESH)

    fetch = pltpu.make_async_copy(fields_hbm, fbuf, fsem)
    fetch.start()
    barrier = pltpu.get_barrier_semaphore()
    unrolled = n <= 32

    def for_peers(first, last, body):
        if unrolled:
            for k in reversed(range(first, last)):
                body(k)
        else:
            lax.fori_loop(first, last, lambda k, c: (body(k), c)[1], 0)

    for_peers(1, n, lambda k: pl.semaphore_signal(
        barrier, inc=1, device_id=peer(k), device_id_type=pl.DeviceIdType.MESH))

    shift_bits = elems.bit_length() - 1
    own = owners_ref[...]
    owner_dev = jnp.right_shift(own, shift_bits)
    local = (own - owner_dev * elems).astype(F32)
    hit = (jnp.bitwise_xor(iota((n, blocks), 0), me) == owner_dev).astype(F32)
    earlier = (iota((blocks, blocks), 0) < iota((blocks, blocks), 1)).astype(F32)
    rank = jnp.dot(hit, earlier, preferred_element_type=F32)
    match = [jnp.where(rank == float(c), hit, 0.0) for c in range(CAP)]
    both = jnp.concatenate(match, axis=0)
    cat = jnp.concatenate([targets_ref[:, a, :] for a in range(3)], axis=1)
    packed = jnp.dot(both, cat, precision=EXACT, preferred_element_type=F32)
    elem_rows = lax.dot_general(both, jnp.broadcast_to(local, (pts, blocks)), NT, preferred_element_type=F32)
    for c in range(CAP):
        part = slice(c * n, (c + 1) * n)
        for a in range(3):
            send[pl.ds(4 * c + a, n, stride=8), :] = packed[part, a * pts:(a + 1) * pts]
        send[pl.ds(4 * c + 3, n, stride=8), :] = elem_rows[part]
        for a in range(3):
            recv[4 * c + a:4 * c + a + 1, :] = packed[c * n:c * n + 1, a * pts:(a + 1) * pts]
        recv[4 * c + 3:4 * c + 4, :] = elem_rows[c * n:c * n + 1]
    square = (blocks, blocks)
    diag = iota(square, 0) == iota(square, 1)
    own_rows = jnp.broadcast_to(own, square)
    own_col = jnp.sum(jnp.where(diag, own_rows, 0), axis=1, keepdims=True)
    dev_col = jnp.right_shift(own_col, shift_bits)
    dev_row = jnp.right_shift(own_rows, shift_bits)
    same = jnp.where(dev_col == dev_row, 1, 0)
    rank_row = jnp.sum(jnp.where(iota(square, 0) < iota(square, 1), same, 0), axis=0, keepdims=True)
    rank_col = jnp.sum(jnp.where(iota(square, 1) < iota(square, 0), same, 0), axis=1, keepdims=True)
    place = jnp.minimum(CAP * jnp.bitwise_xor(owner_dev, me) + rank_row, CAP * n - 1)
    place = jnp.concatenate([place, jnp.zeros((1, pts - blocks), jnp.int32)], axis=1)
    goes = iota((blocks, lanes), 1) == jnp.bitwise_xor(dev_col, me)
    elem_col = own_col - dev_col * elems
    for c in range(CAP):
        mine = jnp.where(goes, jnp.where(rank_col == c, elem_col, 0), 0)
        idsend[c:c + 1, :] = jnp.sum(mine, axis=0, keepdims=True)
    slotv[...] = place
    slot_copy = pltpu.make_async_copy(slotv, slots, slotsem)
    slot_copy.start()

    pl.semaphore_wait(barrier, n - 1)
    for_peers(1, n, lambda k: remote(send, recv, s1, r1, k, k // group_peers).start())
    for_peers(1, n, lambda k: pltpu.make_async_remote_copy(
        src_ref=idsend, dst_ref=idrecv.at[k], send_sem=s0, recv_sem=r0.at[k // group_peers],
        device_id=peer(k), device_id_type=pl.DeviceIdType.MESH).start())

    row, col = iota((24, 24), 0), iota((24, 24), 1)
    both_bits = jnp.bitwise_and(row, col) % 8
    odd = (both_bits + both_bits // 2 + both_bits // 4) % 2
    hada = jnp.where(row // 8 == col // 8, (1 - 2 * odd).astype(F32) * 0.125, 0.0)
    bits = row % 8
    sign = (1 - 2 * ((bits + bits // 2 + bits // 4) % 2)).astype(F32)
    coefs = jnp.dot(hada * sign, shift_ref[...], precision=EXACT, preferred_element_type=F32)
    c_hi = coefs.astype(BF16)
    rest = coefs - c_hi.astype(F32)
    c_mid = rest.astype(BF16)
    c_lo = (rest - c_mid.astype(F32)).astype(BF16)

    fetch.wait()
    low_sub = iota((8, 128), 0) < 4
    low_lane = iota((8, 128), 1) < 64
    keep = low_sub == low_lane

    def split(e, carry):
        parts = []
        for q in range(4):
            x = fbuf[e, :, q * 128:(q + 1) * 128]
            x = jnp.concatenate([x, x], axis=0)
            hi = x.astype(BF16).astype(F32)
            lo = x - hi
            a = jnp.where(low_sub, hi, lo)
            b = pltpu.roll(jnp.where(low_sub, lo, hi), 64, axis=1)
            parts.append(jnp.where(keep, a, b))
        table[e] = jnp.concatenate(parts, axis=0).astype(BF16)
        return carry

    lax.fori_loop(0, elems, split, 0, unroll=4)

    per = group_peers
    count = CAP * per

    def run_group(g, first):
        base = g * per
        got = per - 1 if first else per
        start = base + 1 if first else base
        pltpu.make_async_copy(recv.at[rows(start, got), :], recv.at[rows(start, got), :], r1.at[g]).wait()

        def gather(a):
            return jnp.concatenate(
                [recv[pl.ds(8 * base + 4 * c + a, per, stride=8), :] for c in range(CAP)], axis=0)

        y = [gather(a) for a in range(3)]
        elem = gather(3)
        lane = iota((count, pts), 1)
        if first:
            own_ids = pltpu.make_async_copy(idsend, ids.at[0], idsem)
            own_ids.start()
        taken = idrecv.at[pl.ds(start, got)]
        pltpu.make_async_copy(taken, taken, r0.at[g]).wait()
        id_copy = pltpu.make_async_copy(taken, ids.at[pl.ds(start, got)], idsem2)
        id_copy.start()
        pick = jnp.where(elem[:, :elems] == lane[:, :elems].astype(F32), 1.0, 0.0).astype(BF16)
        chosen = sum(lax.dot_general(pick, c, NT, preferred_element_type=F32) for c in (c_hi, c_mid, c_lo))
        coef = []
        for a in range(3):
            line = []
            for m in range(8):
                value = chosen[:, 8 * a + m:8 * a + m + 1]
                if m == 4 >> a:
                    value = value + 1.0
                line.append(jnp.broadcast_to(value, (count, pts)))
            coef.append(line)
        xi = newton(coef, y)
        for a in range(3):
            for i, value in enumerate(lagrange(xi[a])):
                lag[a, pl.ds(i, count, stride=8), :] = value
        if first:
            own_ids.wait()
        id_copy.wait()
        for s in range(count):
            c, p = s // per, s % per
            e = ids[base + p, c, base + p]
            left = table[e]
            lz = lag[2, 8 * s:8 * s + 8, :]
            w = jnp.concatenate([lag[1, 8 * s + j:8 * s + j + 1, :] * lz for j in range(8)], axis=0)
            w_hi = w.astype(BF16)
            w_lo = (w - w_hi.astype(F32)).astype(BF16)
            prod = jnp.dot(
                jnp.concatenate([left, left], axis=1),
                jnp.concatenate([w_hi, w_hi, w_lo, w_lo], axis=0),
                preferred_element_type=F32)
            total = None
            for q in range(4):
                lx = jnp.where(low_sub, lag[0, 8 * s + 2 * q:8 * s + 2 * q + 1, :],
                               lag[0, 8 * s + 2 * q + 1:8 * s + 2 * q + 2, :])
                term = prod[8 * q:8 * q + 8] * lx
                total = term if total is None else total + term
            total = total[0:4] + total[4:8]
            if first and p == 0:
                ret[c] = total
            else:
                res[CAP * (base + p) + c] = total
        for_peers_in = range(1 if first else 0, per)
        for p in for_peers_in:
            remote(res, ret, s2, r2, base + p, g).start()

    run_group(0, True)
    if unrolled:
        for g in range(1, groups):
            run_group(g, False)
    else:
        lax.fori_loop(1, groups, lambda g, c: (run_group(g, False), c)[1], 0)

    slot_copy.wait()
    rest_rows = rows(1, n - 1)
    for g in range(groups):
        start, got = (1, per - 1) if g == 0 else (g * per, per)
        back = ret.at[pl.ds(CAP * start, CAP * got)]
        pltpu.make_async_copy(back, back, r2.at[g]).wait()
    for b in range(blocks):
        out_ref[b] = ret[slots[0, b]]
    pltpu.make_async_copy(idrecv.at[pl.ds(1, n - 1)], idrecv.at[pl.ds(1, n - 1)], s0).wait()
    pltpu.make_async_copy(send.at[rest_rows, :], send.at[rest_rows, :], s1).wait()
    left = res.at[pl.ds(CAP, CAP * (n - 1))]
    pltpu.make_async_copy(left, left, s2).wait()


def shards(sizes, old_fields, corner_shift, targets, owners):
    n = sizes[0] * sizes[1] * sizes[2]
    elems, nvar, nodes = old_fields.shape
    blocks = owners.shape[0]
    pts = targets.shape[1] // blocks
    assert n & (n - 1) == 0 and elems & (elems - 1) == 0 and nvar == 4 and nodes == 512
    group_peers = min(GROUP_PEERS, n)
    groups = n // group_peers
    lanes = 128 * ((n + 127) // 128)
    points = targets.reshape(3, blocks, pts).transpose(1, 0, 2)
    vmem = pl.BlockSpec(memory_space=pltpu.VMEM)
    message = pltpu.VMEM((8 * n, pts), F32)
    result = pltpu.VMEM((CAP * n, nvar, pts), F32)
    out = pl.pallas_call(
        functools.partial(kernel, sizes, group_peers),
        out_shape=jax.ShapeDtypeStruct((blocks, nvar, pts), F32),
        in_specs=[vmem, vmem, vmem, pl.BlockSpec(memory_space=pl.ANY)],
        out_specs=vmem,
        scratch_shapes=[
            pltpu.VMEM((elems, nvar, nodes), F32),
            pltpu.VMEM((elems, 32, 128), BF16),
            message, message, result, result,
            pltpu.VMEM((3, 8 * CAP * group_peers, pts), F32),
            pltpu.VMEM((CAP, lanes), jnp.int32),
            pltpu.VMEM((n, CAP, lanes), jnp.int32),
            pltpu.SMEM((n, CAP, lanes), jnp.int32),
            pltpu.VMEM((1, pts), jnp.int32),
            pltpu.SMEM((1, pts), jnp.int32),
            pltpu.SemaphoreType.DMA, pltpu.SemaphoreType.DMA, pltpu.SemaphoreType.DMA, pltpu.SemaphoreType.DMA,
            pltpu.SemaphoreType.DMA, pltpu.SemaphoreType.DMA((groups,)),
            pltpu.SemaphoreType.DMA, pltpu.SemaphoreType.DMA((groups,)),
            pltpu.SemaphoreType.DMA, pltpu.SemaphoreType.DMA((groups,)),
        ],
        compiler_params=pltpu.CompilerParams(collective_id=0, has_side_effects=True),
    )(owners.reshape(1, blocks), points, corner_shift, old_fields)
    return out.transpose(1, 0, 2).reshape(nvar, blocks * pts)


def solution(mesh):
    sizes = tuple(mesh.shape[a] for a in AXES)
    in_specs = (
        P(("groups", "block", "seg", "sub"), None, None),
        P(None, ("groups", "block", "seg", "sub")),
        P(None, ("groups", "block", "seg", "sub")),
        P(("groups", "block", "seg", "sub")),
    )
    out_specs = P(None, ("groups", "block", "seg", "sub"))
    return jax.shard_map(functools.partial(shards, sizes), mesh=mesh, in_specs=in_specs,
                         out_specs=out_specs, check_vma=False)
```

time: 65.3 us -> 19 us (0.29)
  starting transfers between devices: 19.6 us -> 0 us
  Pallas kernels: 0 us -> 17.3 us
  waiting for transfers between devices: 15.9 us -> 0 us
  local copies, waits for them, and re-layouts: 12 us -> 1.47 us
  blocking collectives: 8.63 us -> 0 us
  matrix products: 5.16 us -> 0 us
  other arithmetic: 2.71 us -> 0 us
    all_to_all x5 -> x0, starting transfers between devices: 19.6 us -> none  [the longest x1 6.48 us: shards(): lax.all_to_all(wanted.reshape(outer_count, inner_count, CAP), 'block', sp...]
    pallas_call x0 -> x1, Pallas kernels: none -> 17.3 us  [shards(): pl.pallas_call(functools.partial(kernel, sizes, group_peers), out_shape=j...]
    all_to_all x5 -> x0, waiting for transfers between devices: 15.9 us -> none  [the longest x1 4.07 us: shards(): lax.all_to_all(lax.all_to_all(computed.reshape(outer_count, inner_count,...]
    all_to_all x1 -> x0, blocking collectives: 8.63 us -> none  [shards(): lax.all_to_all(computed.reshape(outer_count, inner_count, CAP, var_count,...]
    dot_general x13 -> x0, matrix products: 5.16 us -> none  [the longest x9 3.03 us: invert_map(): jnp.dot(corners, slope_row, precision=EXACT)]
    gather x4 -> x0, local copies, waits for them, and re-layouts: 2.58 us -> none  [the longest x1 1.23 us: shards(): mine = returned.reshape(slot_count, var_count, point_count)[slot_index]]
    all_to_all x7 -> x0, local copies, waits for them, and re-layouts: 2.2 us -> none  [the longest x1 0.68 us: shards(): lax.all_to_all(wanted.reshape(outer_count, inner_count, CAP), 'block', sp...]
    scatter x2 -> x0, local copies, waits for them, and re-layouts: 2.17 us -> none  [the longest x1 1.49 us: shards(): jnp.zeros((slot_count, 3, point_count), jnp.float32).at[slot_index]]
  transfers between devices with their start and end apart: 5 -> 0, of which waited for: 5 -> 0; matrix products, arithmetic and copies ran while one was open for 8% -> 0% of each run, Pallas kernels for 0% -> 0%
where the time goes in v1:
time: 19 us; the launch traced here: 18.8 us
  Pallas kernels  17.3 us (91%)
  local copies, waits for them, and re-layouts  1.47 us (8%)
    pallas_call x1, Pallas kernels, shards(): pl.pallas_call(functools.partial(kernel, sizes, group_peers), out_shape=j...  17.3 us
    unnamed x1, local copies, waits for them, and re-layouts  1.47 us

profile of v1, /device:TPU:0, one launch (start us, length us, event | category | flops | bytes accessed | tf_op | source)
XLA Modules:
  0.0 18.8 jit_solution(14720721119851940749)
XLA Ops:
  0.0 17.3 %shard_map.46 = f32[32,4,128]{2,1,0:T(4,128)} custom-call(s32[1,32]{1,0:T(1,128)} %bitcast.9, f32[32,3,128]{2,1,0:T(4,128)} %bitcast.8, f32[24,64]{1,0:T(8,128)} %shift_ref.1, f32[64,4,512]{2,1,0:T(4,128)} %fields_hbm.1), custom_call_target="tpu_custom_call" | custom-call | tf_op jit(solution)/shard_map/pallas_call | solution.py:328
  17.3 1.5 %copy.6 = f32[4,4096]{1,0:T(4,128)} copy(f32[4,4096]{1,0:T(4,128)} %bitcast.7) | data formatting | bytes 131072

commit v2 on v1

--- a/solution.py
+++ b/solution.py
@@ -96,9 +96,9 @@
     return out
 
 
-def kernel(sizes, group_peers, owners_ref, targets_ref, shift_ref, fields_hbm, out_ref,
-           fbuf, table, send, recv, res, ret, lag, idsend, idrecv, ids, slotv, slots,
-           fsem, idsem, idsem2, slotsem, s0, r0, s1, r1, s2, r2):
+def kernel(sizes, group_peers, owners_hbm, targets_hbm, shift_hbm, fields_hbm, out_ref,
+           owners_ref, targets_ref, shift_ref, fbuf, table, send, recv, res, ret, lag, idsend, idrecv, ids, slotv, slots,
+           osem, tsem, csem, fsem, idsem, slotsem, s0, r0, s1, r1, s2, r2):
     nb, ns, nc = sizes
     n = nb * ns * nc
     blocks = owners_ref.shape[1]
@@ -106,6 +106,7 @@
     pts = out_ref.shape[2]
     groups = n // group_peers
     lanes = idsend.shape[1]
+    wide = idsend.shape[0]
     here = [lax.axis_index(a) for a in AXES]
     me = (here[0] * ns + here[1]) * nc + here[2]
 
@@ -119,17 +120,25 @@
         other = jnp.bitwise_xor(me, k)
         return {"block": other // (ns * nc), "seg": (other // nc) % ns, "sub": other % nc}
 
-    def rows(k, count=1):
-        start = 8 * k
-        return pl.ds(start if isinstance(start, int) else pl.multiple_of(start, 8), 8 * count)
-
-    def remote(src, dst, ssem, rsem, k, g):
-        part = rows(k) if src is send else pl.ds(CAP * k, CAP)
+    def message(k):
+        return pl.ds(8 * k if isinstance(k, int) else pl.multiple_of(8 * k, 8), 3 * CAP)
+
+    def for_wait(first, count, ref, sem):
+        part = ref.at[pl.ds(8 * first, 3 * CAP * count), :]
+        pltpu.make_async_copy(part, part, sem).wait()
+
+    def send_result(k, g):
+        part = pl.ds(CAP * k, CAP)
         return pltpu.make_async_remote_copy(
-            src_ref=src.at[part], dst_ref=dst.at[part],
-            send_sem=ssem, recv_sem=rsem.at[g],
+            src_ref=res.at[part], dst_ref=ret.at[part], send_sem=s2, recv_sem=r2.at[g],
             device_id=peer(k), device_id_type=pl.DeviceIdType.MESH)
 
+    get_owners = pltpu.make_async_copy(owners_hbm, owners_ref, osem)
+    get_owners.start()
+    get_targets = pltpu.make_async_copy(targets_hbm, targets_ref, tsem)
+    get_targets.start()
+    get_shift = pltpu.make_async_copy(shift_hbm, shift_ref, csem)
+    get_shift.start()
     fetch = pltpu.make_async_copy(fields_hbm, fbuf, fsem)
     fetch.start()
     barrier = pltpu.get_barrier_semaphore()
@@ -146,25 +155,22 @@
         barrier, inc=1, device_id=peer(k), device_id_type=pl.DeviceIdType.MESH))
 
     shift_bits = elems.bit_length() - 1
+    get_owners.wait()
     own = owners_ref[...]
     owner_dev = jnp.right_shift(own, shift_bits)
-    local = (own - owner_dev * elems).astype(F32)
     hit = (jnp.bitwise_xor(iota((n, blocks), 0), me) == owner_dev).astype(F32)
     earlier = (iota((blocks, blocks), 0) < iota((blocks, blocks), 1)).astype(F32)
     rank = jnp.dot(hit, earlier, preferred_element_type=F32)
     match = [jnp.where(rank == float(c), hit, 0.0) for c in range(CAP)]
     both = jnp.concatenate(match, axis=0)
+    get_targets.wait()
     cat = jnp.concatenate([targets_ref[:, a, :] for a in range(3)], axis=1)
     packed = jnp.dot(both, cat, precision=EXACT, preferred_element_type=F32)
-    elem_rows = lax.dot_general(both, jnp.broadcast_to(local, (pts, blocks)), NT, preferred_element_type=F32)
     for c in range(CAP):
         part = slice(c * n, (c + 1) * n)
         for a in range(3):
-            send[pl.ds(4 * c + a, n, stride=8), :] = packed[part, a * pts:(a + 1) * pts]
-        send[pl.ds(4 * c + 3, n, stride=8), :] = elem_rows[part]
-        for a in range(3):
-            recv[4 * c + a:4 * c + a + 1, :] = packed[c * n:c * n + 1, a * pts:(a + 1) * pts]
-        recv[4 * c + 3:4 * c + 4, :] = elem_rows[c * n:c * n + 1]
+            send[pl.ds(3 * c + a, n, stride=8), :] = packed[part, a * pts:(a + 1) * pts]
+            recv[3 * c + a:3 * c + a + 1, :] = packed[c * n:c * n + 1, a * pts:(a + 1) * pts]
     square = (blocks, blocks)
     diag = iota(square, 0) == iota(square, 1)
     own_rows = jnp.broadcast_to(own, square)
@@ -176,25 +182,34 @@
     rank_col = jnp.sum(jnp.where(iota(square, 1) < iota(square, 0), same, 0), axis=1, keepdims=True)
     place = jnp.minimum(CAP * jnp.bitwise_xor(owner_dev, me) + rank_row, CAP * n - 1)
     place = jnp.concatenate([place, jnp.zeros((1, pts - blocks), jnp.int32)], axis=1)
-    goes = iota((blocks, lanes), 1) == jnp.bitwise_xor(dev_col, me)
     elem_col = own_col - dev_col * elems
-    for c in range(CAP):
-        mine = jnp.where(goes, jnp.where(rank_col == c, elem_col, 0), 0)
-        idsend[c:c + 1, :] = jnp.sum(mine, axis=0, keepdims=True)
+    lane_of = jnp.where(rank_col < CAP, jnp.bitwise_xor(dev_col, me) + n * rank_col, -1)
+    for r in range(wide):
+        here_lane = iota((blocks, lanes), 1) + lanes * r == lane_of
+        row = jnp.sum(jnp.where(here_lane, elem_col, 0), axis=0, keepdims=True)
+        idsend[r:r + 1, :] = row
+        idrecv[r:r + 1, :] = row
     slotv[...] = place
     slot_copy = pltpu.make_async_copy(slotv, slots, slotsem)
     slot_copy.start()
 
     pl.semaphore_wait(barrier, n - 1)
-    for_peers(1, n, lambda k: remote(send, recv, s1, r1, k, k // group_peers).start())
-    for_peers(1, n, lambda k: pltpu.make_async_remote_copy(
-        src_ref=idsend, dst_ref=idrecv.at[k], send_sem=s0, recv_sem=r0.at[k // group_peers],
-        device_id=peer(k), device_id_type=pl.DeviceIdType.MESH).start())
+    def send_points(k):
+        g = k // group_peers
+        pltpu.make_async_remote_copy(
+            src_ref=idsend, dst_ref=idrecv.at[pl.ds(wide * k, wide), :], send_sem=s0, recv_sem=r0.at[g],
+            device_id=peer(k), device_id_type=pl.DeviceIdType.MESH).start()
+        pltpu.make_async_remote_copy(
+            src_ref=send.at[message(k), :], dst_ref=recv.at[message(k), :], send_sem=s1, recv_sem=r1.at[g],
+            device_id=peer(k), device_id_type=pl.DeviceIdType.MESH).start()
+
+    for_peers(1, n, send_points)
 
     row, col = iota((24, 24), 0), iota((24, 24), 1)
     both_bits = jnp.bitwise_and(row, col) % 8
     odd = (both_bits + both_bits // 2 + both_bits // 4) % 2
     hada = jnp.where(row // 8 == col // 8, (1 - 2 * odd).astype(F32) * 0.125, 0.0)
+    get_shift.wait()
     bits = row % 8
     sign = (1 - 2 * ((bits + bits // 2 + bits // 4) % 2)).astype(F32)
     coefs = jnp.dot(hada * sign, shift_ref[...], precision=EXACT, preferred_element_type=F32)
@@ -230,23 +245,25 @@
         base = g * per
         got = per - 1 if first else per
         start = base + 1 if first else base
-        pltpu.make_async_copy(recv.at[rows(start, got), :], recv.at[rows(start, got), :], r1.at[g]).wait()
+        for_wait(start, got, recv, r1.at[g])
 
         def gather(a):
             return jnp.concatenate(
-                [recv[pl.ds(8 * base + 4 * c + a, per, stride=8), :] for c in range(CAP)], axis=0)
+                [recv[pl.ds(8 * base + 3 * c + a, per, stride=8), :] for c in range(CAP)], axis=0)
 
         y = [gather(a) for a in range(3)]
-        elem = gather(3)
-        lane = iota((count, pts), 1)
-        if first:
-            own_ids = pltpu.make_async_copy(idsend, ids.at[0], idsem)
-            own_ids.start()
-        taken = idrecv.at[pl.ds(start, got)]
+        taken = idrecv.at[pl.ds(wide * start, wide * got), :]
         pltpu.make_async_copy(taken, taken, r0.at[g]).wait()
-        id_copy = pltpu.make_async_copy(taken, ids.at[pl.ds(start, got)], idsem2)
+        id_copy = pltpu.make_async_copy(idrecv.at[pl.ds(wide * base, wide * per), :], ids.at[pl.ds(wide * base, wide * per), :], idsem)
         id_copy.start()
-        pick = jnp.where(elem[:, :elems] == lane[:, :elems].astype(F32), 1.0, 0.0).astype(BF16)
+        id_lane = iota((per, lanes), 1) - iota((per, lanes), 0)
+        id_cols = []
+        for c in range(CAP):
+            at = c * n + base
+            id_rows = idrecv[pl.ds(wide * base + at // lanes, per, stride=wide), :]
+            id_cols.append(jnp.sum(jnp.where(id_lane == at % lanes, id_rows, 0), axis=1, keepdims=True))
+        elem = jnp.concatenate(id_cols, axis=0)
+        pick = jnp.where(elem == iota((count, elems), 1), 1.0, 0.0).astype(BF16)
         chosen = sum(lax.dot_general(pick, c, NT, preferred_element_type=F32) for c in (c_hi, c_mid, c_lo))
         coef = []
         for a in range(3):
@@ -261,12 +278,10 @@
         for a in range(3):
             for i, value in enumerate(lagrange(xi[a])):
                 lag[a, pl.ds(i, count, stride=8), :] = value
-        if first:
-            own_ids.wait()
         id_copy.wait()
         for s in range(count):
             c, p = s // per, s % per
-            e = ids[base + p, c, base + p]
+            e = ids[wide * (base + p) + (c * n + base) // lanes, (c * n + base) % lanes + p]
             left = table[e]
             lz = lag[2, 8 * s:8 * s + 8, :]
             w = jnp.concatenate([lag[1, 8 * s + j:8 * s + j + 1, :] * lz for j in range(8)], axis=0)
@@ -289,7 +304,7 @@
                 res[CAP * (base + p) + c] = total
         for_peers_in = range(1 if first else 0, per)
         for p in for_peers_in:
-            remote(res, ret, s2, r2, base + p, g).start()
+            send_result(base + p, g).start()
 
     run_group(0, True)
     if unrolled:
@@ -299,15 +314,15 @@
         lax.fori_loop(1, groups, lambda g, c: (run_group(g, False), c)[1], 0)
 
     slot_copy.wait()
-    rest_rows = rows(1, n - 1)
     for g in range(groups):
         start, got = (1, per - 1) if g == 0 else (g * per, per)
         back = ret.at[pl.ds(CAP * start, CAP * got)]
         pltpu.make_async_copy(back, back, r2.at[g]).wait()
     for b in range(blocks):
         out_ref[b] = ret[slots[0, b]]
-    pltpu.make_async_copy(idrecv.at[pl.ds(1, n - 1)], idrecv.at[pl.ds(1, n - 1)], s0).wait()
-    pltpu.make_async_copy(send.at[rest_rows, :], send.at[rest_rows, :], s1).wait()
+    rest_ids = idrecv.at[pl.ds(wide, wide * (n - 1)), :]
+    pltpu.make_async_copy(rest_ids, rest_ids, s0).wait()
+    for_wait(1, n - 1, send, s1)
     left = res.at[pl.ds(CAP, CAP * (n - 1))]
     pltpu.make_async_copy(left, left, s2).wait()
 
@@ -320,33 +335,38 @@
     assert n & (n - 1) == 0 and elems & (elems - 1) == 0 and nvar == 4 and nodes == 512
     group_peers = min(GROUP_PEERS, n)
     groups = n // group_peers
-    lanes = 128 * ((n + 127) // 128)
+    wide = (CAP * n + 127) // 128
     points = targets.reshape(3, blocks, pts).transpose(1, 0, 2)
     vmem = pl.BlockSpec(memory_space=pltpu.VMEM)
+    hbm = pl.BlockSpec(memory_space=pltpu.HBM)
     message = pltpu.VMEM((8 * n, pts), F32)
     result = pltpu.VMEM((CAP * n, nvar, pts), F32)
     out = pl.pallas_call(
         functools.partial(kernel, sizes, group_peers),
         out_shape=jax.ShapeDtypeStruct((blocks, nvar, pts), F32),
-        in_specs=[vmem, vmem, vmem, pl.BlockSpec(memory_space=pl.ANY)],
+        in_specs=[hbm] * 4,
         out_specs=vmem,
         scratch_shapes=[
+            pltpu.VMEM((1, blocks), jnp.int32),
+            pltpu.VMEM((blocks, 3, pts), F32),
+            pltpu.VMEM((24, elems), F32),
             pltpu.VMEM((elems, nvar, nodes), F32),
             pltpu.VMEM((elems, 32, 128), BF16),
             message, message, result, result,
             pltpu.VMEM((3, 8 * CAP * group_peers, pts), F32),
-            pltpu.VMEM((CAP, lanes), jnp.int32),
-            pltpu.VMEM((n, CAP, lanes), jnp.int32),
-            pltpu.SMEM((n, CAP, lanes), jnp.int32),
+            pltpu.VMEM((wide, 128), jnp.int32),
+            pltpu.VMEM((wide * n, 128), jnp.int32),
+            pltpu.SMEM((wide * n, 128), jnp.int32),
             pltpu.VMEM((1, pts), jnp.int32),
             pltpu.SMEM((1, pts), jnp.int32),
-            pltpu.SemaphoreType.DMA, pltpu.SemaphoreType.DMA, pltpu.SemaphoreType.DMA, pltpu.SemaphoreType.DMA,
+            *[pltpu.SemaphoreType.DMA] * 6,
             pltpu.SemaphoreType.DMA, pltpu.SemaphoreType.DMA((groups,)),
             pltpu.SemaphoreType.DMA, pltpu.SemaphoreType.DMA((groups,)),
             pltpu.SemaphoreType.DMA, pltpu.SemaphoreType.DMA((groups,)),
         ],
-        compiler_params=pltpu.CompilerParams(collective_id=0, has_side_effects=True),
-    )(owners.reshape(1, blocks), points, corner_shift, old_fields)
+        compiler_params=pltpu.CompilerParams(
+            collective_id=0, has_side_effects=True, vmem_limit_bytes=16 * 1024 * 1024),
+    )(*[pltpu.with_memory_space_constraint(x, pltpu.HBM) for x in (owners.reshape(1, blocks), points, corner_shift, old_fields)])
     return out.transpose(1, 0, 2).reshape(nvar, blocks * pts)
 
 

time: 19 us -> 16.1 us (0.85)
  Pallas kernels: 17.3 us -> 15.3 us
  local copies, waits for them, and re-layouts: 1.47 us -> 0.63 us
    pallas_call x1, Pallas kernels: 17.3 us -> 15.3 us  [shards(): pl.pallas_call(functools.partial(kernel, sizes, group_peers), out_shape=j...]
    unnamed x1, local copies, waits for them, and re-layouts: 1.47 us -> 0.63 us
where the time goes in v2:
time: 16.1 us; the launch traced here: 15.9 us
  Pallas kernels  15.3 us (95%)
  local copies, waits for them, and re-layouts  0.63 us (4%)
    pallas_call x1, Pallas kernels, shards(): pl.pallas_call(functools.partial(kernel, sizes, group_peers), out_shape=j...  15.3 us
    unnamed x1, local copies, waits for them, and re-layouts  0.63 us

profile of v2, /device:TPU:0, one launch (start us, length us, event | category | flops | bytes accessed | tf_op | source)
XLA Modules:
  0.0 15.9 jit_solution(4099716785488666711)
XLA Ops:
  0.0 15.3 %shard_map.46 = f32[32,4,128]{2,1,0:T(4,128)S(1)} custom-call(s32[1,32]{1,0:T(1,128)} %bitcast.9, f32[32,3,128]{2,1,0:T(4,128)} %bitcast.8, f32[24,64]{1,0:T(8,128)} %shift_hbm.1, f32[64,4,512]{2,1,0:T(4,128)} %fields_hbm.1), custom_call_target="tpu_custom_call" | custom-call | tf_op jit(solution)/shard_map/pallas_call | solution.py:344
  15.3 0.6 %copy.6 = f32[4,4096]{1,0:T(4,128)} copy(f32[4,4096]{1,0:T(4,128)S(1)} %bitcast.7) | data formatting | bytes 131072

commit v3 on v2

--- a/solution.py
+++ b/solution.py
@@ -9,7 +9,7 @@
 
 NEWTON = 3
 CAP = 2
-GROUP_PEERS = 8
+GROUP_PEERS = 4
 AXES = ("block", "seg", "sub")
 
 GLL_POINTS = (

time: 16.1 us -> 15.9 us (0.988)
  Pallas kernels: 15.3 us -> 15.1 us
where the time goes in v3:
time: 15.9 us; the launch traced here: 15.8 us
  Pallas kernels  15.1 us (95%)
  local copies, waits for them, and re-layouts  0.63 us (4%)
    pallas_call x1, Pallas kernels, shards(): pl.pallas_call(functools.partial(kernel, sizes, group_peers), out_shape=j...  15.1 us
    unnamed x1, local copies, waits for them, and re-layouts  0.63 us

profile of v3, /device:TPU:0, one launch (start us, length us, event | category | flops | bytes accessed | tf_op | source)
XLA Modules:
  0.0 15.8 jit_solution(11651700092332825014)
XLA Ops:
  0.0 15.1 %shard_map.46 = f32[32,4,128]{2,1,0:T(4,128)S(1)} custom-call(s32[1,32]{1,0:T(1,128)} %bitcast.9, f32[32,3,128]{2,1,0:T(4,128)} %bitcast.8, f32[24,64]{1,0:T(8,128)} %shift_hbm.1, f32[64,4,512]{2,1,0:T(4,128)} %fields_hbm.1), custom_call_target="tpu_custom_call" | custom-call | tf_op jit(solution)/shard_map/pallas_call | solution.py:344
  15.1 0.6 %copy.6 = f32[4,4096]{1,0:T(4,128)} copy(f32[4,4096]{1,0:T(4,128)S(1)} %bitcast.7) | data formatting | bytes 131072
